TPU v7x, 256 devices: a whole 4x4x8 slice. The times are simulated.
256 devices in a mesh: img: 8 (over y, x_lo), cls: 8 (over z), emb: 4 (over x_hi, core).
Axes of the slice: x: 4 (x_hi: 2, x_lo: 2; x = x_hi * 2 + x_lo), y: 4, z: 8, core: 2. Of those that a mesh axis runs over, the one named last changes fastest.
Arguments:
- regions: bfloat16 [8192, 1024], P('img', 'emb'), may hold values from -8 to 8
- table: bfloat16 [21504, 1024], P('cls', 'emb'), may hold values from -1 to 1
- shift: float32 [8192], P('img'), may hold values from -0.5 to 0.1
- scale: float32 [8192], P('img'), may hold values from 2 to 20
- labels: int32 [8192], P('img'), may hold values from -1 to 21503, as said below
- valid: int32 [16, 21504], P('img', 'cls'), may hold values 0 or 1
Outputs:
- loss: float32 [], replicated
- region_grad: bfloat16 [8192, 1024], P('img', 'emb')
- table_grad: bfloat16 [21504, 1024], P('cls', 'emb')
Inputs may be any that keep to these rules, and one draw needn't show every extreme that they name: `labels`: -1 marks background; the first region of every image is foreground.
All inputs are finite; a program needn't handle non-finite values. No bound on the sum of `valid` on one device may be relied on, other than what follows from the above.
Results may differ from a plain program's by a relative error of at most 0.0034.
Values may be sent and summed in bfloat16 or wider, within the bound.
No kernel may reach another device: no remote copies, remote signals or barrier semaphores. Data moves between devices by JAX's collectives and lax.ppermute only.
A program may use at most 64 MiB of HBM per device.

v0:
```python
import functools
import jax
import jax.numpy as jnp
from jax import lax
from jax.sharding import Mesh
from jax.sharding import PartitionSpec as P

CLASSES = 21504
REG_IMG = 512
EMB = ("emb_0", "emb_1")
IMG = ("img_0", "img_1")
IMG_CLS_EMB = ("img_0", "img_1", "cls", "emb_0", "emb_1")


def over_axes(shard, axes):
    return functools.reduce(lax.psum, axes, shard)


def focal(logit, target):
    prob = jax.nn.sigmoid(logit)
    return -0.25 * target * (1.0 - prob) ** 2 * jax.nn.log_sigmoid(logit) - 0.75 * (
        1.0 - target
    ) * prob**2 * jax.nn.log_sigmoid(-logit)


def shards(regions, table, shift, scale, labels, valid):
    rows = regions.shape[0]
    class_dev = table.shape[0]
    parts = lax.axis_size(EMB)
    quarter = rows // parts
    start = lax.axis_index(EMB) * quarter
    block = regions.astype(jnp.float32)
    squares = lax.psum(jnp.sum(block * block, axis=1), EMB)
    local_count = jnp.sum((labels >= 0).astype(jnp.float32))
    count = lax.psum(local_count, IMG)
    inv = lax.rsqrt(squares + 1e-06)
    unit = block * inv[:, None]
    unit_b = unit.astype(jnp.bfloat16)
    unit_rows = lax.all_to_all(unit_b, EMB, split_axis=0, concat_axis=1, tiled=True)
    cosine = lax.dot_general(
        unit_rows,
        lax.all_gather(table, EMB, axis=1, tiled=True),
        (((1,), (1,)), ((), ())),
        preferred_element_type=jnp.float32,
    )
    shift_q = lax.dynamic_slice_in_dim(shift, start, quarter, 0)
    scale_q = lax.dynamic_slice_in_dim(scale, start, quarter, 0)
    label_q = lax.dynamic_slice_in_dim(labels, start, quarter, 0)
    image_ids = (start + jnp.arange(quarter, dtype=jnp.int32)) // REG_IMG
    onehot = (image_ids[:, None] == jnp.arange(valid.shape[0], dtype=jnp.int32)[None, :]).astype(
        jnp.float32
    )
    mask = jnp.dot(onehot, valid.astype(jnp.float32), preferred_element_type=jnp.float32)
    class_ids = lax.axis_index("cls") * class_dev + jnp.arange(class_dev, dtype=jnp.int32)
    logit = (cosine + shift_q[:, None]) * scale_q[:, None]
    target = (label_q[:, None] == class_ids[None, :]).astype(jnp.float32)
    term, pullback = jax.vjp(lambda value: focal(value, target), logit)
    dlogit = pullback(jnp.ones_like(term))[0]
    total = over_axes(jnp.sum(term * mask), IMG_CLS_EMB)
    factor = rows * lax.axis_size(IMG) / count
    dscore = (dlogit * mask * scale_q[:, None] * factor).astype(jnp.bfloat16)
    piece = lax.all_gather(dscore, EMB, axis=0, tiled=True)
    dunit_piece = jnp.dot(piece, table, preferred_element_type=jnp.float32)
    table_acc = lax.dot_general(
        piece, unit_b, (((0,), (0,)), ((), ())), preferred_element_type=jnp.float32
    )
    dunit = lax.psum(dunit_piece, "cls")
    radial = lax.psum(jnp.sum(unit * dunit, axis=1), EMB)
    region_grad = (inv[:, None] * (dunit - unit * radial[:, None])).astype(jnp.bfloat16)
    table_grad = lax.psum(table_acc, IMG).astype(jnp.bfloat16)
    loss = total / count / CLASSES
    return (loss, region_grad, table_grad)


def solution(mesh):
    torus = Mesh(
        mesh.devices.reshape(4, 2, mesh.shape["cls"], 2, 2),
        ("img_0", "img_1", "cls", "emb_0", "emb_1"),
    )
    return jax.shard_map(
        shards,
        mesh=torus,
        in_specs=(P(IMG, EMB), P("cls", EMB), P(IMG), P(IMG), P(IMG), P(IMG, "cls")),
        out_specs=(P(), P(IMG, EMB), P("cls", EMB)),
        check_vma=False,
    )
```

profile of v0, /device:TPU:1, one launch (start us, length us, event | category | flops | bytes accessed | tf_op | source)
XLA Modules:
  0.0 273.6 jit_solution(13197794882755454692)
XLA Ops:
  7.2 0.0 copy-start.2
  7.2 0.0 all-gather.3.cloned.1.call-start
  7.2 0.7 all-gather.3.cloned.1.call-update
  7.9 1.3 fusion.33
  9.2 9.7 %psum.70 = f32[1024]{0:T(1024)S(1)} all-reduce(f32[1024]{0:T(1024)S(1)} %fusion.33), channel_id=1, replica_groups=mesh['img_0'=4,'img_1'=2,'cls'=8,'emb_0'=2,'emb_1'=2] {'emb_0','emb_1'}, use_global_device_ids=true, to_apply=%region_1.0 | all-reduce | flops 1024 | bytes 8192 | tf_op jit(solution)/shard_map/psum | solution.py:33
  18.9 1.2 fusion.28
  20.2 1.0 copy.9
  21.2 5.2 %all-to-all-start = ((bf16[4,256,256]{1,2,0:T(8,128)(2,1)}), bf16[4,256,256]{1,2,0:T(8,128)(2,1)S(1)}, u32[]{:S(2)}, u32[]{:S(2)}) async-start(bf16[4,256,256]{1,2,0:T(8,128)(2,1)} %copy.9), calls=%async_computation | async-start | bytes 1048576 | tf_op jit(solution)/shard_map/all_to_all | solution.py:39
  26.3 0.0 all-gather.5.cloned.1.call-start
  26.3 0.0 copy-done.2
  26.3 0.6 convert_reduce_fusion
  26.9 24.0 %psum.76 = f32[]{:T(128)} all-reduce(f32[]{:T(128)} %convert_reduce_fusion), channel_id=1, replica_groups=mesh['img_0'=4,'img_1'=2,'cls'=8,'emb_0'=2,'emb_1'=2] {'img_0','img_1'}, use_global_device_ids=true, to_apply=%region_9.11 | all-reduce | flops 1 | bytes 8 | tf_op jit(solution)/shard_map/psum | solution.py:35
  51.0 0.1 dynamic_slice.9
  51.0 0.8 dynamic_slice.11
  51.8 0.8 dynamic_slice.10
  53.3 0.0 all-to-all-done
  53.3 15.6 %all-gather.3.cloned.1.call-done = bf16[2688,1024]{1,0:T(8,128)(2,1)} async-done(((bf16[2688,256]{1,0:T(8,128)(2,1)}), bf16[2688,1024]{1,0:T(8,128)(2,1)}) %all-gather.3.cloned.1.call-update) | async-done | bytes 5505040 | tf_op jit(solution)/shard_map/all_gather | solution.py:42
  68.9 0.0 copy-start.3
  68.9 4.5 %fusion = f32[256,2688]{1,0:T(8,128)S(1)} fusion(bf16[256,1024]{0,1:T(8,128)(2,1)S(1)} %bitcast.11, bf16[2688,1024]{1,0:T(8,128)(2,1)} %all-gather.3.cloned.1.call-done, f32[256]{0:T(256)S(1)} %dynamic_slice.11, f32[256]{0:T(256)S(1)} %dynamic_slice.10), kind=kOutput, calls=%fused_computation.7 | convolution fusion | flops 1410662400 | bytes 8783872 | tf_op jit(solution)/shard_map/dot_general | solution.py:40
  73.4 0.0 copy-done.3
  73.4 0.0 copy-start.1
  73.4 9.8 %fusion.12 = (bf16[256,2688]{1,0:T(8,128)(2,1)}, f32[]{:T(128)}) fusion(f32[256,2688]{1,0:T(8,128)S(1)} %fusion, f32[]{:T(128)S(6)} %div.31, f32[256]{0:T(256)S(1)} %dynamic_slice.11, s32[2688]{0:T(1024)S(1)} %iota_add_fusion, s32[256]{0:T(256)S(1)} %dynamic_slice.9, s32[2,2688]{1,0:T(2,128)S(1)} %copy-done.3, s32[256]{0:T(256)S(1)} %and_select_fusion), kind=kOutput, calls=%fused_computation.25 | convolution fusion | flops 47486720 | bytes 4164104 | tf_op jit(solution)/shard_map/dot_general | solution.py:53
  83.2 0.0 all-gather.5.cloned.1.call-update
  83.3 0.0 all-reduce.3.cloned.1.call-start
  83.3 9.4 %psum.71 = f32[]{:T(128)} all-reduce(f32[]{:T(128)} %get-tuple-element.12), channel_id=1, replica_groups=mesh['img_0'=4,'img_1'=2,'cls'=8,'emb_0'=2,'emb_1'=2] {'img_0'}, use_global_device_ids=true, to_apply=%region_3.5 | all-reduce | flops 1 | bytes 8 | tf_op jit(solution)/shard_map/psum | solution.py:16
  92.7 4.4 %psum.72 = f32[]{:T(128)} all-reduce(f32[]{:T(128)} %psum.71), channel_id=1, replica_groups=mesh['img_0'=4,'img_1'=2,'cls'=8,'emb_0'=2,'emb_1'=2] {'img_1'}, use_global_device_ids=true, to_apply=%region_4.6 | all-reduce | flops 1 | bytes 8 | tf_op jit(solution)/shard_map/psum | solution.py:16
  97.1 16.2 %psum.73 = f32[]{:T(128)} all-reduce(f32[]{:T(128)} %psum.72), channel_id=1, replica_groups=mesh['img_0'=4,'img_1'=2,'cls'=8,'emb_0'=2,'emb_1'=2] {'cls'}, use_global_device_ids=true, to_apply=%region_5.7 | all-reduce | flops 1 | bytes 8 | tf_op jit(solution)/shard_map/psum | solution.py:16
  113.3 6.5 %psum.74 = f32[]{:T(128)} all-reduce(f32[]{:T(128)} %psum.73), channel_id=1, replica_groups=mesh['img_0'=4,'img_1'=2,'cls'=8,'emb_0'=2,'emb_1'=2] {'emb_0'}, use_global_device_ids=true, to_apply=%region_6.8 | all-reduce | flops 1 | bytes 8 | tf_op jit(solution)/shard_map/psum | solution.py:16
  119.8 9.1 %psum.75 = f32[]{:T(128)} all-reduce(f32[]{:T(128)} %psum.74), channel_id=1, replica_groups=mesh['img_0'=4,'img_1'=2,'cls'=8,'emb_0'=2,'emb_1'=2] {'emb_1'}, use_global_device_ids=true, to_apply=%region_7.9 | all-reduce | flops 1 | bytes 8 | tf_op jit(solution)/shard_map/psum | solution.py:16
  130.2 1.8 all-gather.5.cloned.1.call-done
  132.0 0.0 copy-done.1
  132.0 5.2 %fusion.37 = f32[1024,256]{1,0:T(8,128)} fusion(bf16[1024,2688]{1,0:T(8,128)(2,1)} %all-gather.5.cloned.1.call-done, bf16[2688,256]{1,0:T(8,128)(2,1)S(1)} %copy-done.1), kind=kOutput, calls=%fused_computation.63 | convolution fusion | flops 1409286144 | bytes 7929856 | tf_op jit(solution)/shard_map/dot_general | solution.py:63
  137.2 0.0 all-reduce.3.cloned.1.call-update
  137.3 4.2 %fusion.38 = f32[2688,256]{1,0:T(8,128)S(1)} fusion(bf16[1024,2688]{1,0:T(8,128)(2,1)} %all-gather.5.cloned.1.call-done, bf16[1024,256]{1,0:T(8,128)(2,1)S(1)} %fusion.28), kind=kOutput, calls=%fused_computation.64 | convolution fusion | flops 1409286144 | bytes 8781824 | tf_op jit(solution)/shard_map/dot_general | solution.py:64
  141.5 0.0 copy-start
  141.5 111.4 %all-reduce.4 = bf16[2688,256]{1,0:T(8,128)(2,1)} all-reduce(f32[2688,256]{1,0:T(8,128)S(1)} %fusion.38), channel_id=1, replica_groups=mesh['img_0'=4,'img_1'=2,'cls'=8,'emb_0'=2,'emb_1'=2] {'img_0','img_1'}, use_global_device_ids=true, to_apply=%region_13.15 | all-reduce | flops 688128 | bytes 4128768 | tf_op jit(solution)/shard_map/psum | solution.py:70
  253.0 0.0 all-reduce.3.cloned.1.call-done
  253.0 0.0 copy-done
  253.0 1.6 fusion.29
  254.6 9.0 %psum.78 = f32[1024]{0:T(1024)S(1)} all-reduce(f32[1024]{0:T(1024)S(1)} %fusion.29), channel_id=1, replica_groups=mesh['img_0'=4,'img_1'=2,'cls'=8,'emb_0'=2,'emb_1'=2] {'emb_0','emb_1'}, use_global_device_ids=true, to_apply=%region_12.14 | all-reduce | flops 1024 | bytes 8192 | tf_op jit(solution)/shard_map/psum | solution.py:68
  263.5 2.4 fusion.32
  (3 shorter events, 0.0 us)
Async XLA Ops:
  7.2 19.2 %copy-start.2 = (s32[1024]{0:T(1024)S(1)}, s32[1024]{0:T(1024)}, u32[]{:S(2)}) copy-start(s32[1024]{0:T(1024)} %param.11) | copy-start | bytes 12292
  7.2 61.7 %all-gather.3.cloned.1.call-start = ((), (), s32[]{:S(2)}) async-start(), calls=%async_computation.1 | async-start | bytes 6881280 | tf_op jit(solution)/shard_map/all_gather | solution.py:42
  21.2 32.1 %all-to-all-start = ((bf16[4,256,256]{1,2,0:T(8,128)(2,1)}), bf16[4,256,256]{1,2,0:T(8,128)(2,1)S(1)}, u32[]{:S(2)}, u32[]{:S(2)}) async-start(bf16[4,256,256]{1,2,0:T(8,128)(2,1)} %copy.9), calls=%async_computation | async-start | bytes 1048576 | tf_op jit(solution)/shard_map/all_to_all | solution.py:39
  26.3 105.7 %all-gather.5.cloned.1.call-start = ((), (), s32[]{:S(2)}) async-start(), calls=%async_computation.2 | async-start | bytes 6881280 | tf_op jit(solution)/shard_map/all_gather | solution.py:62
  68.9 4.5 %copy-start.3 = (s32[2,2688]{1,0:T(2,128)S(1)}, s32[2,2688]{1,0:T(2,128)}, u32[]{:S(2)}) copy-start(s32[2,2688]{1,0:T(2,128)} %param.12) | copy-start | bytes 64516
  73.4 58.6 %copy-start.1 = (bf16[2688,256]{1,0:T(8,128)(2,1)S(1)}, bf16[2688,256]{1,0:T(8,128)(2,1)}, u32[]{:S(2)}) copy-start(bf16[2688,256]{1,0:T(8,128)(2,1)} %param.8) | copy-start | bytes 4128772
  83.3 169.7 %all-reduce.3.cloned.1.call-start = ((), (), s32[]{:S(2)}) async-start(), calls=%async_computation.3 | async-start | bytes 2097152 | tf_op jit(solution)/shard_map/psum | solution.py:67
  141.5 111.5 %copy-start = (bf16[1024,256]{1,0:T(8,128)(2,1)S(1)}, bf16[1024,256]{1,0:T(8,128)(2,1)}, u32[]{:S(2)}) copy-start(bf16[1024,256]{1,0:T(8,128)(2,1)} %param.7) | copy-start | bytes 1572868
Sparse Core Ops, SparseCore 0:
  9.8 59.0 all-gather.2
  83.4 48.5 all-gather.4
  137.4 70.8 all-reduce.2
where the time goes:
time: 274 us
  blocking collectives  200 us (73%)
  matrix products  23.8 us (9%)
  waiting for transfers between devices  18.1 us (7%)
  between operations  17 us (6%)
  other arithmetic  7.09 us (3%)
  starting transfers between devices  5.23 us (2%)
    psum x1, blocking collectives, shards(): table_grad = lax.psum(table_acc, IMG).astype(jnp.bfloat16)  111 us
    psum x5, blocking collectives, over_axes(): return functools.reduce(lax.psum, axes, shard)  45.6 us
    psum x1, blocking collectives, shards(): count = lax.psum(local_count, IMG)  24 us
    all_gather x1, waiting for transfers between devices, shards(): lax.all_gather(table, EMB, axis=1, tiled=True)  15.6 us
    dot_general x1, matrix products, shards(): jnp.dot(onehot, valid.astype(jnp.float32), preferred_element_type=jnp.flo...  9.78 us
    psum x1, blocking collectives, shards(): squares = lax.psum(jnp.sum(block * block, axis=1), EMB)  9.73 us
    psum x1, blocking collectives, shards(): radial = lax.psum(jnp.sum(unit * dunit, axis=1), EMB)  8.96 us
  transfers between devices with their start and end apart: 4, of which 2 were waited for; matrix products, arithmetic and copies ran while one was open for 4% of the time, Pallas kernels for 0%

commit v1 on v0

--- a/solution.py
+++ b/solution.py
@@ -67,7 +67,7 @@
     dunit = lax.psum(dunit_piece, "cls")
     radial = lax.psum(jnp.sum(unit * dunit, axis=1), EMB)
     region_grad = (inv[:, None] * (dunit - unit * radial[:, None])).astype(jnp.bfloat16)
-    table_grad = lax.psum(table_acc, IMG).astype(jnp.bfloat16)
+    table_grad = jnp.sum(lax.all_gather(table_acc, IMG), axis=0).astype(jnp.bfloat16)
     loss = total / count / CLASSES
     return (loss, region_grad, table_grad)
 

time: 274 us -> 657 us (2.40)
  waiting for transfers between devices: 18.1 us -> 499 us
  blocking collectives: 200 us -> 90.2 us
  other arithmetic: 7.09 us -> 16.8 us
    all_gather x0 -> x1, waiting for transfers between devices: none -> 415 us  [shards(): lax.all_gather(table_acc, IMG)]
    psum x1 -> x0, blocking collectives: 111 us -> none  [shards(): table_grad = lax.psum(table_acc, IMG).astype(jnp.bfloat16)]
    all_gather x1, waiting for transfers between devices: 1.81 us -> 48.6 us  [shards(): piece = lax.all_gather(dscore, EMB, axis=0, tiled=True)]
    psum x1, waiting for transfers between devices: 0.01 us -> 19 us  [shards(): dunit = lax.psum(dunit_piece, 'cls')]
    reduce_sum x0 -> x1, other arithmetic: none -> 9.7 us  [shards(): jnp.sum(lax.all_gather(table_acc, IMG), axis=0).astype(jnp.bfloat16)]
  transfers between devices with their start and end apart: 4 -> 5, of which waited for: 2 -> 4; matrix products, arithmetic and copies ran while one was open for 4% -> 2% of each run, Pallas kernels for 0% -> 0%
where the time goes in v1:
time: 657 us; the launch traced here: 656 us
  waiting for transfers between devices  499 us (76%)
  blocking collectives  90.2 us (14%)
  matrix products  25.2 us (4%)
  between operations  17 us (3%)
  other arithmetic  16.8 us (3%)
    all_gather x1, waiting for transfers between devices, shards(): lax.all_gather(table_acc, IMG)  415 us
    all_gather x1, waiting for transfers between devices, shards(): piece = lax.all_gather(dscore, EMB, axis=0, tiled=True)  48.6 us
    psum x5, blocking collectives, over_axes(): return functools.reduce(lax.psum, axes, shard)  44.8 us
    psum x1, blocking collectives, shards(): count = lax.psum(local_count, IMG)  24 us
    psum x1, waiting for transfers between devices, shards(): dunit = lax.psum(dunit_piece, 'cls')  19 us
    all_gather x1, waiting for transfers between devices, shards(): lax.all_gather(table, EMB, axis=1, tiled=True)  15.6 us
  transfers between devices with their start and end apart: 5, of which 4 were waited for; matrix products, arithmetic and copies ran while one was open for 2% of the time, Pallas kernels for 0%

profile of v1, /device:TPU:1, one launch (start us, length us, event | category | flops | bytes accessed | tf_op | source)
XLA Modules:
  0.0 656.2 jit_solution(6289224377994652833)
XLA Ops:
  7.2 0.0 copy-start.2
  7.2 0.0 all-gather.5.cloned.1.call-start
  7.2 0.7 all-gather.5.cloned.1.call-update
  7.9 1.3 fusion.33
  9.2 9.7 %psum.63 = f32[1024]{0:T(1024)S(1)} all-reduce(f32[1024]{0:T(1024)S(1)} %fusion.33), channel_id=1, replica_groups=mesh['img_0'=4,'img_1'=2,'cls'=8,'emb_0'=2,'emb_1'=2] {'emb_0','emb_1'}, use_global_device_ids=true, to_apply=%region_1.0 | all-reduce | flops 1024 | bytes 8192 | tf_op jit(solution)/shard_map/psum | solution.py:33
  18.9 1.2 fusion.28
  20.2 1.0 copy.9
  21.2 5.2 all-to-all-start
  26.3 0.0 all-gather.7.cloned.1.call-start
  26.3 0.0 copy-done.2
  26.3 0.6 convert_reduce_fusion
  26.9 24.0 %psum.69 = f32[]{:T(128)} all-reduce(f32[]{:T(128)} %convert_reduce_fusion), channel_id=1, replica_groups=mesh['img_0'=4,'img_1'=2,'cls'=8,'emb_0'=2,'emb_1'=2] {'img_0','img_1'}, use_global_device_ids=true, to_apply=%region_9.11 | all-reduce | flops 1 | bytes 8 | tf_op jit(solution)/shard_map/psum | solution.py:35
  51.0 0.1 dynamic_slice.9
  51.0 0.8 dynamic_slice.11
  51.8 0.8 dynamic_slice.10
  53.3 0.0 all-to-all-done
  53.3 15.6 %all-gather.5.cloned.1.call-done = bf16[2688,1024]{1,0:T(8,128)(2,1)} async-done(((bf16[2688,256]{1,0:T(8,128)(2,1)}), bf16[2688,1024]{1,0:T(8,128)(2,1)}) %all-gather.5.cloned.1.call-update) | async-done | bytes 5505040 | tf_op jit(solution)/shard_map/all_gather | solution.py:42
  68.9 0.0 copy-start.3
  68.9 4.5 fusion
  73.4 0.0 copy-done.3
  73.4 0.0 copy-start.1
  73.4 9.8 %fusion.12 = (bf16[256,2688]{1,0:T(8,128)(2,1)}, f32[]{:T(128)}) fusion(f32[256,2688]{1,0:T(8,128)S(1)} %fusion, f32[]{:T(128)S(6)} %div.31, f32[256]{0:T(256)S(1)} %dynamic_slice.11, s32[2688]{0:T(1024)S(1)} %iota_add_fusion, s32[256]{0:T(256)S(1)} %dynamic_slice.9, s32[2,2688]{1,0:T(2,128)S(1)} %copy-done.3, s32[256]{0:T(256)S(1)} %and_select_fusion), kind=kOutput, calls=%fused_computation.25 | convolution fusion | flops 47486720 | bytes 4164104 | tf_op jit(solution)/shard_map/dot_general | solution.py:53
  83.2 0.0 all-gather.7.cloned.1.call-update
  83.3 0.0 all-reduce.2.cloned.1.call-start
  83.3 48.6 %all-gather.7.cloned.1.call-done = bf16[1024,2688]{1,0:T(8,128)(2,1)} async-done(((bf16[256,2688]{1,0:T(8,128)(2,1)}), bf16[1024,2688]{1,0:T(8,128)(2,1)}) %all-gather.7.cloned.1.call-update) | async-done | bytes 5505040 | tf_op jit(solution)/shard_map/all_gather | solution.py:62
  131.9 0.0 copy-done.1
  131.9 5.2 fusion.37
  137.1 0.0 all-reduce.2.cloned.1.call-update
  137.1 0.0 all-gather.9.cloned.1.call-start
  137.2 5.7 fusion.38
  142.9 0.0 copy-start
  142.9 0.0 all-gather.9.cloned.1.call-update
  142.9 9.5 %psum.64 = f32[]{:T(128)} all-reduce(f32[]{:T(128)} %get-tuple-element.12), channel_id=1, replica_groups=mesh['img_0'=4,'img_1'=2,'cls'=8,'emb_0'=2,'emb_1'=2] {'img_0'}, use_global_device_ids=true, to_apply=%region_3.5 | all-reduce | flops 1 | bytes 8 | tf_op jit(solution)/shard_map/psum | solution.py:16
  152.4 4.4 psum.65
  156.8 15.6 %psum.66 = f32[]{:T(128)} all-reduce(f32[]{:T(128)} %psum.65), channel_id=1, replica_groups=mesh['img_0'=4,'img_1'=2,'cls'=8,'emb_0'=2,'emb_1'=2] {'cls'}, use_global_device_ids=true, to_apply=%region_5.7 | all-reduce | flops 1 | bytes 8 | tf_op jit(solution)/shard_map/psum | solution.py:16
  172.4 5.9 psum.67
  178.3 9.4 %psum.68 = f32[]{:T(128)} all-reduce(f32[]{:T(128)} %psum.67), channel_id=1, replica_groups=mesh['img_0'=4,'img_1'=2,'cls'=8,'emb_0'=2,'emb_1'=2] {'emb_1'}, use_global_device_ids=true, to_apply=%region_7.9 | all-reduce | flops 1 | bytes 8 | tf_op jit(solution)/shard_map/psum | solution.py:16
  189.1 19.0 %all-reduce.2.cloned.1.call-done = f32[1024,256]{1,0:T(8,128)} async-done(((f32[1024,256]{1,0:T(8,128)}), f32[1024,256]{1,0:T(8,128)}) %all-reduce.2.cloned.1.call-update) | async-done | bytes 1048592 | tf_op jit(solution)/shard_map/psum | solution.py:67
  208.0 0.0 copy-done
  208.0 1.6 fusion.29
  209.6 11.7 %psum.71 = f32[1024]{0:T(1024)S(1)} all-reduce(f32[1024]{0:T(1024)S(1)} %fusion.29), channel_id=1, replica_groups=mesh['img_0'=4,'img_1'=2,'cls'=8,'emb_0'=2,'emb_1'=2] {'emb_0','emb_1'}, use_global_device_ids=true, to_apply=%region_12.14 | all-reduce | flops 1024 | bytes 8192 | tf_op jit(solution)/shard_map/psum | solution.py:68
  221.3 2.4 fusion.32
  223.7 415.1 %all-gather.9.cloned.1.call-done = f32[21504,256]{1,0:T(8,128)} async-done(((f32[2688,256]{1,0:T(8,128)}), f32[21504,256]{1,0:T(8,128)}) %all-gather.9.cloned.1.call-update) | async-done | bytes 22020112 | tf_op jit(solution)/shard_map/all_gather | solution.py:70
  638.8 9.7 %reduce_sum.49 = bf16[2688,256]{1,0:T(8,128)(2,1)} reduce(f32[8,2688,256]{2,1,0:T(8,128)} %bitcast.11, f32[]{:T(128)} %constant.52.clone.1), dimensions={0}, to_apply=%region_13.15 | reduce | flops 4816896 | bytes 23396356 | tf_op jit(solution)/shard_map/reduce_sum | solution.py:70
  (3 shorter events, 0.0 us)
Async XLA Ops:
  7.2 19.2 %copy-start.2 = (s32[1024]{0:T(1024)S(1)}, s32[1024]{0:T(1024)}, u32[]{:S(2)}) copy-start(s32[1024]{0:T(1024)} %param.11) | copy-start | bytes 12292
  7.2 61.7 %all-gather.5.cloned.1.call-start = ((), (), s32[]{:S(2)}) async-start(), calls=%async_computation.1 | async-start | bytes 6881280 | tf_op jit(solution)/shard_map/all_gather | solution.py:42
  21.2 32.1 %all-to-all-start = ((bf16[4,256,256]{1,2,0:T(8,128)(2,1)}), bf16[4,256,256]{1,2,0:T(8,128)(2,1)S(1)}, u32[]{:S(2)}, u32[]{:S(2)}) async-start(bf16[4,256,256]{1,2,0:T(8,128)(2,1)} %copy.9), calls=%async_computation | async-start | bytes 1048576 | tf_op jit(solution)/shard_map/all_to_all | solution.py:39
  26.3 105.6 %all-gather.7.cloned.1.call-start = ((), (), s32[]{:S(2)}) async-start(), calls=%async_computation.2 | async-start | bytes 6881280 | tf_op jit(solution)/shard_map/all_gather | solution.py:62
  68.9 4.5 copy-start.3
  73.4 58.5 %copy-start.1 = (bf16[2688,256]{1,0:T(8,128)(2,1)S(1)}, bf16[2688,256]{1,0:T(8,128)(2,1)}, u32[]{:S(2)}) copy-start(bf16[2688,256]{1,0:T(8,128)(2,1)} %param.8) | copy-start | bytes 4128772
  83.3 124.8 %all-reduce.2.cloned.1.call-start = ((), (), s32[]{:S(2)}) async-start(), calls=%async_computation.3 | async-start | bytes 2097152 | tf_op jit(solution)/shard_map/psum | solution.py:67
  137.1 501.7 %all-gather.9.cloned.1.call-start = ((), (), s32[]{:S(2)}) async-start(), calls=%async_computation.4 | async-start | bytes 24772608 | tf_op jit(solution)/shard_map/all_gather | solution.py:70
  142.9 65.1 %copy-start = (bf16[1024,256]{1,0:T(8,128)(2,1)S(1)}, bf16[1024,256]{1,0:T(8,128)(2,1)}, u32[]{:S(2)}) copy-start(bf16[1024,256]{1,0:T(8,128)(2,1)} %param.7) | copy-start | bytes 1572868
Sparse Core Ops, SparseCore 0:
  9.8 59.0 all-gather.4
  83.4 48.5 all-gather.6
  137.3 70.7 all-reduce.1
  209.7 429.1 all-gather.8
